TPU v7x, 256 devices: a 8x8x2 block of a 8x8x16 slice. The times are simulated.
256 devices in a mesh: group: 2 (over z), dp: 16 (over y, core), tensor: 8 (over x).
Axes of the slice: x: 8, y: 8, z: 2, core: 2. Of those that a mesh axis runs over, the one named last changes fastest.
The devices are a block of a 8x8x16 slice.
Arguments:
- tokens: bfloat16 [4096, 5120], P(('group', 'dp'), 'tensor'), parts along dimension 0, may hold values from -6 to 6
- router: bfloat16 [5120, 8], replicated, may hold values from -0.078125 to 0.078125
- expert_gate: bfloat16 [5120, 32768], P(None, ('dp', 'tensor')), may hold values from -0.078125 to 0.078125
- expert_up: bfloat16 [5120, 32768], P(None, ('dp', 'tensor')), may hold values from -0.078125 to 0.078125
- expert_down: bfloat16 [32768, 5120], P(('dp', 'tensor')), may hold values from -0.09375 to 0.09375
- shared_gate: bfloat16 [5120, 4096], P('dp', 'tensor'), may hold values from -0.078125 to 0.078125
- shared_up: bfloat16 [5120, 4096], P('dp', 'tensor'), may hold values from -0.078125 to 0.078125
- shared_down: bfloat16 [4096, 5120], P('tensor', 'dp'), may hold values from -0.09375 to 0.09375
- expert_ids: int32 [4096], P(('group', 'dp')), parts along dimension 0, may hold values from 0 to 7, as said below
- expert_slots: int32 [4096], P(('group', 'dp')), parts along dimension 0, may hold values from 0 to 31, as said below
Outputs:
- mixed: bfloat16 [4096, 5120], P(('group', 'dp'), 'tensor'), parts along dimension 0
There are 2 independent parts, one for each index of `group`. A program takes and returns all parts, laid end to end along the dimension named above; an argument that names none is the same for every part. Nothing has to cross between parts.
Inputs may be any that keep to these rules, and one draw needn't show every extreme that they name: `expert_ids`: among the tokens of one index of dp no expert has more than 32; in every draw one expert has exactly 32 tokens from every index of dp. `expert_slots`: tokens of one index of dp with the same expert have distinct slots.
All inputs are finite; a program needn't handle non-finite values.
Results may differ from a plain program's by a relative error of at most 0.015.
Values may be sent and summed in bfloat16 or wider, within the bound.
A program may use at most 128 MiB of HBM per device.

v0:
```python
import jax
import jax.numpy as jnp
from jax import lax
from jax.sharding import PartitionSpec as P


def joined_along(tiles, dim):
    dims = list(tiles.shape[1:])
    dims[dim] *= tiles.shape[0]
    return jnp.moveaxis(tiles, 0, dim).reshape(dims)


def copy_for_each(value, axis):
    copies = jnp.broadcast_to(value, (lax.axis_size(axis), *value.shape))
    return lax.all_to_all(copies, axis, split_axis=0, concat_axis=0, tiled=True)


def gather_directly(value, axis, dim):
    return joined_along(copy_for_each(value, axis), dim)


def side_by_side(arrays, axis, dim, along):
    both = jnp.concatenate(arrays, axis=along)
    out, at, finished = (lax.all_gather(both, axis, axis=dim, tiled=True), 0, [])
    for a in arrays:
        finished.append(lax.slice_in_dim(out, at, at + a.shape[along], axis=along))
        at += a.shape[along]
    return tuple(finished)


def split_up(value, dim, devices):
    before, after = (value.shape[:dim], value.shape[dim + 1 :])
    return jnp.moveaxis(value.reshape(*before, devices, -1, *after), dim, 0)


def sum_at_owner(value, axis, dim):
    tiles = split_up(value, dim, lax.axis_size(axis))
    arrived = lax.all_to_all(tiles, axis, split_axis=0, concat_axis=0, tiled=True)
    return arrived.astype(jnp.float32).sum(axis=0)


def swapped(value, axis, bit):
    mask = 2**bit
    pairs = [(source, source ^ mask) for source in range(lax.axis_size(axis))]
    return lax.ppermute(value, axis, pairs)


def on_device(
    tokens,
    router,
    expert_gate,
    expert_up,
    expert_down,
    shared_gate,
    shared_up,
    shared_down,
    expert_ids,
    expert_slots,
):
    tok_rows, part_width = tokens.shape
    dp_count = lax.axis_size("dp")
    experts = dp_count // 2
    capacity = min(2 * tok_rows // experts, tok_rows // 2)
    gathered = gather_directly(tokens, "tensor", 1)
    logits = jnp.dot(gathered, router, preferred_element_type=jnp.float32)
    one_hot = (expert_ids[:, None] == jnp.arange(experts, dtype=jnp.int32)[None, :]).astype(
        jnp.float32
    )
    gating = jax.nn.sigmoid(jnp.sum(logits * one_hot, axis=1))
    routed = (tokens.astype(jnp.float32) * gating[:, None]).astype(jnp.bfloat16)
    outgoing = (
        jnp.zeros((experts, capacity, part_width), jnp.bfloat16)
        .at[expert_ids, expert_slots]
        .set(routed)
    )
    pieces = side_by_side((shared_gate, shared_up), "dp", 0, 1)
    gate_sum = jnp.dot(gathered, pieces[0], preferred_element_type=jnp.float32)
    up_sum = jnp.dot(gathered, pieces[1], preferred_element_type=jnp.float32)
    shared_hidden = (jax.nn.silu(gate_sum) * up_sum).astype(jnp.bfloat16)
    shared_terms = jnp.dot(
        shared_hidden,
        lax.all_gather(shared_down, "dp", axis=1, tiled=True),
        preferred_element_type=jnp.float32,
    )
    shared_out = lax.psum_scatter(
        shared_terms.astype(jnp.bfloat16), "tensor", scatter_dimension=1, tiled=True
    ).astype(jnp.float32)
    half_cap = capacity // 2
    to_send = outgoing.reshape(dp_count, half_cap, part_width)
    own_half = lax.all_to_all(to_send, "dp", split_axis=0, concat_axis=0, tiled=True)
    partner = swapped(own_half, "dp", 0)
    parity = lax.axis_index("dp") % 2
    odd_host = parity == 1
    lower_half = jnp.where(odd_host, partner, own_half)
    upper_half = jnp.where(odd_host, own_half, partner)
    received = jnp.concatenate([lower_half, upper_half], axis=1)
    source_count = received.shape[0]
    slot_count = received.shape[1]
    slot_total = source_count * slot_count
    portion = lax.all_gather(received, "tensor", axis=2, tiled=True)
    flattened = portion.reshape(slot_total, portion.shape[2])
    gate_e = jnp.dot(flattened, expert_gate, preferred_element_type=jnp.float32)
    up_e = jnp.dot(flattened, expert_up, preferred_element_type=jnp.float32)
    hidden_e = (jax.nn.silu(gate_e) * up_e).astype(jnp.bfloat16)
    expert_terms = jnp.dot(hidden_e, expert_down, preferred_element_type=jnp.float32)
    expert_terms = expert_terms.reshape(source_count, slot_count, expert_terms.shape[1])
    partials = sum_at_owner(expert_terms.astype(jnp.bfloat16), "tensor", 2)
    partner_sum = swapped(partials.astype(jnp.bfloat16), "dp", 0).astype(partials.dtype)
    paired = partials + partner_sum
    kept_half = lax.dynamic_slice_in_dim(paired, parity * half_cap, half_cap, 1).astype(
        jnp.bfloat16
    )
    returned_raw = lax.all_to_all(kept_half, "dp", split_axis=0, concat_axis=0, tiled=True)
    returned = returned_raw.reshape(experts, capacity, part_width)
    expert_out = returned[expert_ids, expert_slots]
    return (shared_out + expert_out.astype(jnp.float32)).astype(jnp.bfloat16)


def solution(mesh):
    in_specs = (
        P(("group", "dp"), "tensor"),
        P(),
        P(None, ("dp", "tensor")),
        P(None, ("dp", "tensor")),
        P(("dp", "tensor"), None),
        P("dp", "tensor"),
        P("dp", "tensor"),
        P("tensor", "dp"),
        P(("group", "dp")),
        P(("group", "dp")),
    )
    out_specs = P(("group", "dp"), "tensor")
    return jax.shard_map(
        on_device, mesh=mesh, in_specs=in_specs, out_specs=out_specs, check_vma=False
    )
```

profile of v0, /device:TPU:513, one launch (start us, length us, event | category | flops | bytes accessed | tf_op | source)
XLA Modules:
  0.0 341.9 jit_solution(5509344661017308061)
XLA Ops:
  6.5 0.0 copy-start
  6.6 0.0 copy-start.4
  6.6 0.0 copy-start.5
  6.6 0.0 copy-start.3
  6.6 1.2 copy.12
  7.8 0.0 copy-start.2
  7.8 1.3 broadcast_in_dim.8
  9.0 7.9 %all-to-all-start = ((bf16[8,128,640]{1,2,0:T(8,128)(2,1)}), bf16[8,128,640]{1,2,0:T(8,128)(2,1)}, u32[]{:S(2)}, u32[]{:S(2)}) async-start(bf16[8,128,640]{1,2,0:T(8,128)(2,1)} %broadcast_in_dim.8), calls=%async_computation | async-start | bytes 2621440 | tf_op jit(solution)/shard_map/all_to_all | solution.py:15
  16.9 0.1 all-gather.8.cloned.1.call-start
  17.0 0.0 copy-done.4
  17.0 0.0 copy-done.5
  17.0 20.6 %all-to-all-done = bf16[8,128,640]{1,2,0:T(8,128)(2,1)} async-done(((bf16[8,128,640]{1,2,0:T(8,128)(2,1)}), bf16[8,128,640]{1,2,0:T(8,128)(2,1)}, u32[]{:S(2)}, u32[]{:S(2)}) %all-to-all-start) | async-done | bytes 1310752 | tf_op jit(solution)/shard_map/all_to_all | solution.py:15
  37.6 0.0 copy-done.3
  37.6 1.6 fusion.17
  39.2 0.0 copy-done.2
  39.2 0.1 multiply_convert_fusion
  39.4 8.0 %scatter_fusion = bf16[8,32,640]{2,1,0:T(8,128)(2,1)S(1)} fusion(bf16[8,32,640]{2,1,0:T(8,128)(2,1)S(1)} %broadcast_in_dim.18, s32[128]{0:T(128)S(1)} %get-tuple-element.8, bf16[128,640]{1,0:T(8,128)(2,1)S(1)} %multiply_convert_fusion), kind=kCustom, calls=%fused_computation.1 | custom fusion | bytes 492544 | tf_op jit(solution)/shard_map/scatter | solution.py:74
  47.4 40.7 %all_to_all.20 = bf16[16,16,640]{2,1,0:T(8,128)(2,1)S(1)} all-to-all(bf16[16,16,640]{2,1,0:T(8,128)(2,1)S(1)} %bitcast.60), channel_id=1, replica_groups=mesh['group'=2,'dp'=16,'tensor'=8] {'dp'}, dimensions={0} | all-to-all | bytes 655360 | tf_op jit(solution)/shard_map/all_to_all | solution.py:90
  88.1 0.0 collective-permute-start
  88.1 1.6 collective-permute-done
  89.7 0.1 broadcast_select_fusion.1
  89.8 0.9 pad_maximum_fusion.1
  90.7 0.1 all-gather.8.cloned.1.call-update
  90.7 0.1 all-gather.4.cloned.1.call-start
  90.8 2.0 pad_maximum_fusion
  92.8 0.1 all-gather.4.cloned.1.call-update
  92.9 0.1 all-gather.6.cloned.1.call-start
  92.9 0.7 all-gather.6.cloned.1.call-update
  93.7 64.2 %all-gather.8.cloned.1.call-done = bf16[16,32,5120]{2,1,0:T(8,128)(2,1)} async-done(((bf16[16,32,640]{2,1,0:T(8,128)(2,1)}), bf16[16,32,5120]{2,1,0:T(8,128)(2,1)}) %all-gather.8.cloned.1.call-update) | async-done | bytes 5242896 | tf_op jit(solution)/shard_map/all_gather | solution.py:100
  157.9 4.8 %fusion.40 = f32[512,256]{1,0:T(8,128)S(1)} fusion(bf16[512,5120]{1,0:T(8,128)(2,1)} %bitcast.65, bf16[5120,256]{1,0:T(8,128)(2,1)} %param.12), kind=kOutput, calls=%fused_computation.52 | convolution fusion | flops 1342177280 | bytes 8388608 | tf_op jit(solution)/shard_map/dot_general | solution.py:102
  162.7 0.0 copy-done
  162.7 11.2 %convolution_convert_fusion = bf16[512,5120]{1,0:T(8,128)(2,1)} fusion(bf16[256,5120]{1,0:T(8,128)(2,1)S(1)} %copy-done, bf16[512,5120]{1,0:T(8,128)(2,1)} %bitcast.66, bf16[5120,256]{1,0:T(8,128)(2,1)} %param.13, f32[512,256]{1,0:T(8,128)S(1)} %fusion.40), kind=kOutput, calls=%fused_computation.3 | convolution fusion | flops 2687762432 | bytes 16252928 | tf_op jit(solution)/shard_map/dot_general | solution.py:105
  173.9 3.7 %copy.16 = bf16[64,8,8,640]{3,2,1,0:T(8,128)(2,1)S(1)} copy(bf16[64,8,8,640]{3,1,2,0:T(8,128)(2,1)} %bitcast.62) | data formatting | bytes 10485760
  177.6 3.1 copy.18
  180.7 4.9 %all-to-all-start.2 = ((bf16[8,16,32,640]{3,2,1,0:T(8,128)(2,1)}), bf16[8,16,32,640]{3,2,1,0:T(8,128)(2,1)}, u32[]{:S(2)}, u32[]{:S(2)}) async-start(bf16[8,16,32,640]{3,2,1,0:T(8,128)(2,1)} %bitcast.58), calls=%async_computation.2 | async-start | bytes 10485760 | tf_op jit(solution)/shard_map/all_to_all | solution.py:38
  185.6 0.2 reduce-scatter.4.cloned.1.call-start
  185.9 40.7 %all-gather.4.cloned.1.call-done = bf16[5120,1024]{1,0:T(8,128)(2,1)} async-done(((bf16[320,1024]{1,0:T(8,128)(2,1)}), bf16[5120,1024]{1,0:T(8,128)(2,1)}) %all-gather.4.cloned.1.call-update) | async-done | bytes 10485776 | tf_op jit(solution)/shard_map/all_gather | solution.py:24
  226.6 4.4 %fusion.5 = f32[128,512]{0,1:T(8,128)S(1)} fusion(bf16[128,5120]{0,1:T(8,128)(2,1)} %bitcast.1, bf16[5120,1024]{1,0:T(8,128)(2,1)} %all-gather.4.cloned.1.call-done), kind=kOutput, calls=%fused_computation.12 | convolution fusion | flops 671088640 | bytes 6815744 | tf_op jit(solution)/shard_map/dot_general | solution.py:77
  231.0 40.7 %all-gather.6.cloned.1.call-done = bf16[512,5120]{0,1:T(8,128)(2,1)} async-done(((bf16[512,320]{0,1:T(8,128)(2,1)}), bf16[512,5120]{0,1:T(8,128)(2,1)}) %all-gather.6.cloned.1.call-update) | async-done | bytes 5242896 | tf_op jit(solution)/shard_map/all_gather | solution.py:82
  271.7 11.2 %convolution_convert_fusion.1 = bf16[128,5120]{1,0:T(8,128)(2,1)} fusion(bf16[512,5120]{0,1:T(8,128)(2,1)} %all-gather.6.cloned.1.call-done, bf16[128,5120]{0,1:T(8,128)(2,1)} %bitcast.1, bf16[5120,1024]{1,0:T(8,128)(2,1)} %all-gather.4.cloned.1.call-done, f32[128,512]{0,1:T(8,128)S(1)} %fusion.5), kind=kOutput, calls=%fused_computation.4 | convolution fusion | flops 1343225856 | bytes 13369344 | tf_op jit(solution)/shard_map/dot_general | solution.py:80
  282.9 2.4 copy.14
  285.3 0.1 reduce-scatter.4.cloned.1.call-update
  285.4 18.0 %all-to-all-done.2 = bf16[8,16,32,640]{3,2,1,0:T(8,128)(2,1)} async-done(((bf16[8,16,32,640]{3,2,1,0:T(8,128)(2,1)}), bf16[8,16,32,640]{3,2,1,0:T(8,128)(2,1)}, u32[]{:S(2)}, u32[]{:S(2)}) %all-to-all-start.2) | async-done | bytes 5242912 | tf_op jit(solution)/shard_map/all_to_all | solution.py:38
  303.4 3.4 %convert_reduce_fusion = f32[16,32,640]{2,1,0:T(8,128)S(1)} fusion(bf16[8,16,32,640]{3,2,1,0:T(8,128)(2,1)} %all-to-all-done.2), kind=kLoop, calls=%fused_computation.2 | loop fusion | flops 4915200 | bytes 6553600 | tf_op jit(solution)/shard_map/reduce_sum | solution.py:39
  306.8 0.0 copy-start.1
  306.8 1.1 copy-done.1
  307.9 0.1 convert_element_type.53
  308.0 1.1 collective-permute-start.1
  309.1 1.9 collective-permute-done.1
  311.0 2.0 fusion.20
  312.9 7.4 %all-to-all-start.3 = ((bf16[16,16,640]{2,1,0:T(8,128)(2,1)}), bf16[16,16,640]{2,1,0:T(8,128)(2,1)S(1)}, u32[]{:S(2)}, u32[]{:S(2)}) async-start(bf16[16,16,640]{2,1,0:T(8,128)(2,1)} %fusion.20), calls=%async_computation.3 | async-start | bytes 655360 | tf_op jit(solution)/shard_map/all_to_all | solution.py:113
  320.3 2.9 reduce-scatter.4.cloned.1.call-done
  323.2 1.1 copy.15
  324.3 9.0 %all-to-all-done.3 = bf16[16,16,640]{2,1,0:T(8,128)(2,1)S(1)} async-done(((bf16[16,16,640]{2,1,0:T(8,128)(2,1)}), bf16[16,16,640]{2,1,0:T(8,128)(2,1)S(1)}, u32[]{:S(2)}, u32[]{:S(2)}) %all-to-all-start.3) | async-done | bytes 327712 | tf_op jit(solution)/shard_map/all_to_all | solution.py:113
  333.3 1.4 gather_fusion
  334.7 0.7 add_convert_fusion
  (3 shorter events, 0.0 us)
Async XLA Ops:
  6.5 156.2 %copy-start = (bf16[256,5120]{1,0:T(8,128)(2,1)S(1)}, bf16[256,5120]{1,0:T(8,128)(2,1)}, u32[]{:S(2)}) copy-start(bf16[256,5120]{1,0:T(8,128)(2,1)} %param.14) | copy-start | bytes 7864324
  6.6 10.4 %copy-start.4 = (s32[128]{0:T(128)S(1)}, s32[128]{0:T(128)}, u32[]{:S(2)}) copy-start(s32[128]{0:T(128)} %param.18) | copy-start | bytes 1540
  6.6 10.4 %copy-start.5 = (s32[128]{0:T(128)S(1)}, s32[128]{0:T(128)}, u32[]{:S(2)}) copy-start(s32[128]{0:T(128)} %param.19) | copy-start | bytes 1540
  6.6 31.0 %copy-start.3 = (bf16[5120,8]{0,1:T(8,128)(2,1)S(1)}, bf16[5120,8]{0,1:T(8,128)(2,1)}, u32[]{:S(2)}) copy-start(bf16[5120,8]{0,1:T(8,128)(2,1)} %param.11) | copy-start | bytes 245764
  7.8 31.4 %copy-start.2 = (bf16[128,640]{1,0:T(8,128)(2,1)S(1)}, bf16[128,640]{1,0:T(8,128)(2,1)}, u32[]{:S(2)}) copy-start(bf16[128,640]{1,0:T(8,128)(2,1)} %param.10) | copy-start | bytes 491524
  9.0 28.5 %all-to-all-start = ((bf16[8,128,640]{1,2,0:T(8,128)(2,1)}), bf16[8,128,640]{1,2,0:T(8,128)(2,1)}, u32[]{:S(2)}, u32[]{:S(2)}) async-start(bf16[8,128,640]{1,2,0:T(8,128)(2,1)} %broadcast_in_dim.8), calls=%async_computation | async-start | bytes 2621440 | tf_op jit(solution)/shard_map/all_to_all | solution.py:15
  16.9 141.0 %all-gather.8.cloned.1.call-start = ((), (), s32[]{:S(2)}) async-start(), calls=%async_computation.7 | async-start | bytes 5898240 | tf_op jit(solution)/shard_map/all_gather | solution.py:100
  88.1 1.6 collective-permute-start
  90.7 135.9 %all-gather.4.cloned.1.call-start = ((), (), s32[]{:S(2)}) async-start(), calls=%async_computation.5 | async-start | bytes 11141120 | tf_op jit(solution)/shard_map/all_gather | solution.py:24
  92.9 178.9 %all-gather.6.cloned.1.call-start = ((), (), s32[]{:S(2)}) async-start(), calls=%async_computation.6 | async-start | bytes 5570560 | tf_op jit(solution)/shard_map/all_gather | solution.py:82
  180.7 122.7 %all-to-all-start.2 = ((bf16[8,16,32,640]{3,2,1,0:T(8,128)(2,1)}), bf16[8,16,32,640]{3,2,1,0:T(8,128)(2,1)}, u32[]{:S(2)}, u32[]{:S(2)}) async-start(bf16[8,16,32,640]{3,2,1,0:T(8,128)(2,1)} %bitcast.58), calls=%async_computation.2 | async-start | bytes 10485760 | tf_op jit(solution)/shard_map/all_to_all | solution.py:38
  185.6 137.6 %reduce-scatter.4.cloned.1.call-start = ((), (), s32[]{:S(2)}) async-start(), calls=%async_computation.8 | async-start | bytes 1474560
  306.8 1.1 copy-start.1
  308.0 3.0 collective-permute-start.1
  312.9 20.3 %all-to-all-start.3 = ((bf16[16,16,640]{2,1,0:T(8,128)(2,1)}), bf16[16,16,640]{2,1,0:T(8,128)(2,1)S(1)}, u32[]{:S(2)}, u32[]{:S(2)}) async-start(bf16[16,16,640]{2,1,0:T(8,128)(2,1)} %fusion.20), calls=%async_computation.3 | async-start | bytes 655360 | tf_op jit(solution)/shard_map/all_to_all | solution.py:113
Sparse Core Ops, SparseCore 0:
  90.8 66.9 all-gather.7
  159.7 66.8 all-gather.3
  228.5 43.1 all-gather.5
  285.5 37.6 reduce-scatter.3
where the time goes:
time: 343 us; the launch traced here: 342 us
  waiting for transfers between devices  200 us (58%)
  blocking collectives  40.7 us (12%)
  matrix products  33.2 us (10%)
  local copies, waits for them, and re-layouts  23.2 us (7%)
  starting transfers between devices  21.7 us (6%)
  between operations  13.3 us (4%)
  other arithmetic  9.27 us (3%)
    all_gather x1, waiting for transfers between devices, on_device(): portion = lax.all_gather(received, 'tensor', axis=2, tiled=True)  64.2 us
    all_gather x1, waiting for transfers between devices, side_by_side(): lax.all_gather(both, axis, axis=dim, tiled=True)  40.7 us
    all_to_all x1, blocking collectives, on_device(): lax.all_to_all(to_send, 'dp', split_axis=0, concat_axis=0, tiled=True)  40.7 us
    all_gather x1, waiting for transfers between devices, on_device(): lax.all_gather(shared_down, 'dp', axis=1, tiled=True)  40.7 us
    all_to_all x1, waiting for transfers between devices, copy_for_each(): return lax.all_to_all(copies, axis, split_axis=0, concat_axis=0, tiled=True)  20.6 us
    all_to_all x1, waiting for transfers between devices, sum_at_owner(): lax.all_to_all(tiles, axis, split_axis=0, concat_axis=0, tiled=True)  18 us
    dot_general x1, matrix products, on_device(): jnp.dot(hidden_e, expert_down, preferred_element_type=jnp.float32)  11.2 us
    dot_general x1, matrix products, on_device(): jnp.dot(shared_hidden, lax.all_gather(shared_down, 'dp', axis=1, tiled=Tr...  11.2 us
  transfers between devices with their start and end apart: 9, of which 9 were waited for; matrix products, arithmetic and copies ran while one was open for 14% of the time, Pallas kernels for 0%

commit v1 on v0

v1 whole, which is shorter than its diff:
```python
import functools

import jax
import jax.numpy as jnp
from jax import lax
from jax.experimental import pallas as pl
from jax.experimental.pallas import tpu as pltpu
from jax.sharding import PartitionSpec as P

MESH = pl.DeviceIdType.MESH
BF16 = jnp.bfloat16
F32 = jnp.float32


def dot(a, b):
    return jnp.dot(a, b, preferred_element_type=F32)


def dot_turned(a, b):
    return lax.dot_general(a, b, (((1,), (1,)), ((), ())), preferred_element_type=F32)


class Sems:
    def __init__(self, send, recv, local):
        self.send, self.recv, self.local = send, recv, local
        self.used, self.local_used, self.started = 0, 0, []

    def number(self):
        self.used += 1
        return self.used - 1

    def copy(self, number, src, dst, device):
        return pltpu.make_async_remote_copy(
            src_ref=src,
            dst_ref=dst,
            send_sem=self.send.at[number],
            recv_sem=self.recv.at[number],
            device_id=device,
            device_id_type=MESH,
        )

    def start(self, number, src, dst, device):
        copy = self.copy(number, src, dst, device)
        copy.start()
        self.started.append(copy)

    def arrived(self, number, dst, device):
        self.copy(number, dst, dst, device).wait_recv()

    def load(self, src, dst):
        copy = pltpu.make_async_copy(src, dst, self.local.at[self.local_used])
        self.local_used += 1
        copy.start()
        return copy


class Gather:
    def __init__(self, sems, n, me, device_of, region, partner=None):
        self.sems, self.n, self.me, self.half = sems, n, me, n // 2
        self.device_of, self.region, self.partner = device_of, region, partner
        self.numbers = {(k, way, part): sems.number() for k, way, part in self.steps()}
        if partner is not None:
            self.relays = {step: sems.number() for step in [(0, 1, 0), (0, 1, 1), *self.steps()]}

    def carries(self, k, way, part):
        return k < self.half or (k == self.half and part == (0 if way == 1 else 1))

    def steps(self):
        return [
            (k, way, part)
            for k in range(1, self.half + 1)
            for part in (0, 1)
            for way in (1, -1)
            if self.carries(k, way, part)
        ]

    def at(self, offset):
        return lax.rem(self.me + offset + self.n, self.n)

    def send(self, k, way, part):
        if self.carries(k, way, part):
            ref = self.region(self.at(-way * (k - 1)), part, False)
            self.sems.start(self.numbers[k, way, part], ref, ref, self.device_of(self.at(way)))

    def relay(self, k, way, part):
        ref = self.region(self.at(-way * k), part, False)
        self.sems.start(self.relays[k, way, part], ref, ref, self.partner)

    def take(self, k, way, part):
        if self.carries(k, way, part):
            ref = self.region(self.at(-way * k), part, False)
            self.sems.arrived(self.numbers[k, way, part], ref, self.device_of(self.at(-way)))
            if self.partner is not None:
                self.relay(k, way, part)

    def take_on(self, k, part):
        for way in (1, -1):
            if self.carries(k, way, part):
                self.take(k, way, part)
                self.send(k + 1, way, part)

    def relayed(self, k, way):
        for part in (0, 1):
            if k == 0 or self.carries(k, way, part):
                ref = self.region(self.at(-way * k), part, True)
                self.sems.arrived(self.relays[k, way, part], ref, self.partner)


def kernel(
    sizes,
    ids_ref,
    slots_ref,
    tok_hbm,
    router_hbm,
    eg_hbm,
    eu_hbm,
    ed_hbm,
    sg_hbm,
    su_hbm,
    sd_hbm,
    out_ref,
    tok,
    router,
    eg,
    eu,
    ed,
    sg,
    su,
    sd,
    outgoing,
    slot,
    gate_acc,
    up_acc,
    logit_acc,
    hidden,
    own_sum,
    pair_send,
    pair_recv,
    ring_send,
    ring_recv,
    back_send,
    back_recv,
    sgate_acc,
    sup_acc,
    shidden,
    shared_recv,
    shared_send,
    send_sems,
    recv_sems,
    local_sems,
):
    nx, ny, cap = sizes
    half = nx // 2
    toks, width = out_ref.shape
    rows = ny * cap
    part_rows = rows // 2
    krows = sg_hbm.shape[0]
    x = lax.axis_index("tensor")
    d = lax.axis_index("dp")
    core = lax.rem(d, 2)
    y = lax.div(d, 2)
    other = 1 - core
    partner = {"dp": 2 * y + other}
    along_x = lambda i: {"tensor": i}
    along_y = lambda i: {"dp": 2 * i + core}
    at_x = lambda o: lax.rem(x + o + nx, nx)
    at_y = lambda o: lax.rem(y + o + ny, ny)
    sems = Sems(send_sems, recv_sems, local_sems)

    load_tok = sems.load(tok_hbm, tok.at[x])
    my_k = pl.ds(pl.multiple_of(core * krows, krows), krows)
    load_g = sems.load(sg_hbm, sg.at[y, my_k])
    load_u = sems.load(su_hbm, su.at[y, my_k])
    load_d = sems.load(sd_hbm, sd.at[y, my_k])
    load_e = [sems.load(router_hbm, router), sems.load(eg_hbm, eg), sems.load(eu_hbm, eu)]
    load_ed = [sems.load(ed_hbm.at[:, i * width : (i + 1) * width], ed.at[i]) for i in range(nx)]

    barrier = pltpu.get_barrier_semaphore()
    peers = [along_x(at_x(o)) for o in range(1, nx)] + [along_y(at_y(o)) for o in range(1, ny)] + [partner]
    for peer in peers:
        pl.semaphore_signal(barrier, inc=1, device_id=peer, device_id_type=MESH)

    index = ids_ref[...] * cap + slots_ref[...]
    pick = (lax.broadcasted_iota(jnp.int32, (rows, toks), 0) == index).astype(F32).astype(BF16)
    load_tok.wait()
    outgoing[...] = dot(pick, tok[x]).astype(BF16).reshape(ny, cap, width)

    def source_rows(source, of_core):
        return pl.ds(pl.multiple_of(of_core * rows + source * cap, cap), cap)

    slot[x, source_rows(y, core), :] = outgoing[y]

    def core_half(extent, part, swap):
        base = (other if swap else core) * extent + part * (extent // 2)
        return pl.ds(pl.multiple_of(base, extent // 2), extent // 2)

    tok_ring = Gather(
        sems, nx, x, along_x, lambda i, part, swap: tok.at[i, pl.ds(part * (toks // 2), toks // 2)]
    )
    slot_ring = Gather(
        sems, nx, x, along_x, lambda i, part, swap: slot.at[i, core_half(rows, part, swap)], partner
    )

    def wide(i, part, swap):
        base = (other if swap else core) * krows
        return (su if part else sg).at[i, pl.ds(pl.multiple_of(base, krows), krows)]

    wide_ring = Gather(sems, ny, y, along_y, wide, partner)
    def tall(i, part, swap):
        base = (other if swap else core) * krows + part * (krows // 2)
        return sd.at[i, pl.ds(pl.multiple_of(base, krows // 2), krows // 2)]

    down_ring = Gather(sems, ny, y, along_y, tall, partner)
    both = (1, -1)

    far_first = sorted(range(1, ny), key=lambda o: -min(o, ny - o))
    dispatch = {o: sems.number() for o in range(1, ny)}
    back = {o: sems.number() for o in range(1, ny)}
    pl.semaphore_wait(barrier, len(peers))

    for o in far_first:
        sems.start(
            dispatch[o], outgoing.at[at_y(o)], slot.at[x, source_rows(y, core)], along_y(at_y(o))
        )
    for part in (0, 1):
        for way in both:
            tok_ring.send(1, way, part)
    for part, load in ((0, load_g), (1, load_u)):
        load.wait()
        for way in both:
            wide_ring.send(1, way, part)
        wide_ring.relay(0, 1, part)

    for part in (0, 1):
        tok_ring.take_on(1, part)
    load_d.wait()
    for part in (0, 1):
        for way in both:
            down_ring.send(1, way, part)
        down_ring.relay(0, 1, part)
    for k in range(2, half):
        for part in (0, 1):
            tok_ring.take_on(k, part)

    for o in range(1, ny):
        sems.arrived(dispatch[o], slot.at[x, source_rows(at_y(-o), core)], along_y(at_y(-o)))
    for part in (0, 1):
        for way in both:
            slot_ring.send(1, way, part)
        slot_ring.relay(0, 1, part)
    for part in (0, 1):
        tok_ring.take_on(half, part)

    for load in load_e:
        load.wait()

    def expert_chunk(i, first=False):
        at = pl.ds(pl.multiple_of(i * width, width), width)
        terms = (dot(slot[i], eg[at, :]), dot(slot[i], eu[at, :]), dot_turned(slot[i], router[:, at]))
        for acc, term in zip((gate_acc, up_acc, logit_acc), terms):
            acc[...] = term if first else acc[...] + term

    def shared_chunk(i, first=False):
        for acc, weight in ((sgate_acc, sg), (sup_acc, su)):
            term = dot(tok[i], weight[i])
            acc[...] = term if first else acc[...] + term

    slot_ring.relayed(0, 1)
    expert_chunk(x, True)
    wide_ring.relayed(0, 1)
    shared_chunk(y, True)

    def take_slots(k):
        for part in (0, 1):
            slot_ring.take_on(k, part)

    def multiply_slots(k):
        for way in both:
            slot_ring.relayed(k, way)
        for way in both if k < half else (1,):
            expert_chunk(at_x(-way * k))

    def multiply_wide(k):
        for way in both:
            wide_ring.relayed(k, way)
        for way in both if k < half else (1,):
            shared_chunk(at_y(-way * k))

    wide_ring.take_on(1, 0)
    take_slots(1)
    wide_ring.take_on(1, 1)
    multiply_slots(1)
    if half > 2:
        take_slots(2)
        wide_ring.take_on(2, 0)
        multiply_wide(1)
        multiply_slots(2)
    for k in range(3, half):
        take_slots(k)
        wide_ring.take_on(k - 1, 1)
        multiply_slots(k)
    take_slots(half)
    multiply_slots(half)

    lane = lax.broadcasted_iota(jnp.int32, logit_acc.shape, 1)
    logit = jnp.sum(jnp.where(lane == y, logit_acc[...], 0.0), axis=1, keepdims=True)
    factor = jax.nn.sigmoid(logit)
    gate_value = gate_acc[...] * factor
    hidden[...] = (jax.nn.silu(gate_value) * (up_acc[...] * factor)).astype(BF16)
    for load in load_ed:
        load.wait()

    offsets = [half] + [way * k for k in range(half - 1, 0, -1) for way in both] + [0]
    pairs = [sems.number() for _ in offsets]
    hops = {
        (k, way, part): sems.number()
        for k in range(1, half + 1)
        for way in both
        for part in (0, 1)
        if k < half or part == (0 if way == 1 else 1)
    }
    keep_slots = pl.ds(pl.multiple_of(core * rows, rows), rows)
    give_slots = pl.ds(pl.multiple_of(other * rows, rows), rows)
    direction = {1: 0, -1: 1}

    def down_block(at):
        block = ed[at_x(offsets[at])]
        pair_send[at] = dot(hidden[give_slots, :], block).astype(BF16)
        sems.start(pairs[at], pair_send.at[at], pair_recv.at[at], partner)
        own_sum[at] = dot(hidden[keep_slots, :], block)

    def arrived_hop(k, way, part):
        ref = ring_recv.at[direction[way], k - 1, pl.ds(part * part_rows, part_rows)]
        sems.arrived(hops[k, way, part], ref, along_x(at_x(-way)))
        return ref[...].astype(F32)

    def pass_on(at, part):
        offset = offsets[at]
        k = abs(offset)
        part_at = pl.ds(part * part_rows, part_rows)
        value = own_sum[at, part_at, :] + pair_recv[at, part_at, :].astype(F32)
        if offset == 0:
            for way in both:
                value += arrived_hop(1, way, part)
            back_send[part_at, :] = value.astype(BF16)
            return
        way = (1 if part == 0 else -1) if k == half else (1 if offset > 0 else -1)
        if k < half and (k + 1, way, part) in hops:
            value += arrived_hop(k + 1, way, part)
        place = (direction[way], k - 1, part_at)
        ring_send[place] = value.astype(BF16)
        sems.start(hops[k, way, part], ring_send.at[place], ring_recv.at[place], along_x(at_x(way)))

    def paired(at):
        sems.arrived(pairs[at], pair_recv.at[at], partner)

    down_block(0)
    down_block(1)
    paired(0)
    for part in (0, 1):
        pass_on(0, part)
    down_block(2)
    for k in range(2, half):
        wide_ring.take_on(k, 0) if k > 2 or half == 2 else None
    for at in range(3, len(offsets)):
        down_block(at)
    for at in range(1, len(offsets)):
        paired(at)
    for part in (0, 1):
        pass_on(1, part)
        pass_on(2, 1 - part)
    if half > 2:
        wide_ring.take_on(half - 1, 1)
        multiply_wide(half - 2)
    if half > 2:
        for part in (0, 1):
            pass_on(3, part)
            pass_on(4, part)
        multiply_wide(half - 1)
    else:
        multiply_wide(1)
    for way in both:
        for part in (0, 1):
            down_ring.take(1, way, part)
            down_ring.send(2, way, part)
    for part in (0, 1):
        wide_ring.take_on(half, part)
    for k in range(half - 3, 0, -1):
        at = 1 + 2 * (half - 1 - k)
        for part in (0, 1):
            pass_on(at, part)
            pass_on(at + 1, part)
    multiply_wide(half)
    shidden[...] = (jax.nn.silu(sgate_acc[...]) * sup_acc[...]).astype(BF16)

    out_sent = [sems.number() for _ in range(ny)]
    out_came = [sems.number() for _ in range(nx)]
    shared_copies = []

    def shared_block(offset):
        place = at_y(offset)
        value = dot_turned(shidden[...], sd[place]).astype(BF16)
        shared_send[place] = value
        copy = pltpu.make_async_remote_copy(
            src_ref=shared_send.at[place],
            dst_ref=shared_recv.at[x],
            send_sem=send_sems.at[out_sent[offset + ny // 2]],
            recv_sem=recv_sems.at[out_came[0] + x],
            device_id=along_x(place),
            device_id_type=MESH,
        )
        pl.when(place != x)(copy.start)
        shared_copies.append((place, copy))

    def down_blocks(k):
        for way in both if 0 < k < ny // 2 else (1,):
            if k:
                down_ring.relayed(k, way)
                if k == ny // 2:
                    down_ring.relayed(k, -1)
            else:
                down_ring.relayed(0, 1)
            shared_block(-way * k)

    down_blocks(0)
    down_blocks(1)
    for k in range(2, half):
        for part in (0, 1):
            down_ring.take_on(k, part)
        down_blocks(k)
    for part in (0, 1):
        pass_on(len(offsets) - 1, part)
    for o in far_first:
        sems.start(
            back[o], back_send.at[pl.ds(pl.multiple_of(at_y(o) * cap, cap), cap)], back_recv.at[y], along_y(at_y(o))
        )
    back_recv[y] = back_send[pl.ds(pl.multiple_of(y * cap, cap), cap), :]
    for part in (0, 1):
        down_ring.take_on(half, part)
    down_blocks(half)
    total = shared_send[x].astype(F32)

    for o in range(1, ny):
        sems.arrived(back[o], back_recv.at[at_y(-o)], along_y(at_y(-o)))
    total += lax.dot_general(
        pick, back_recv[...].reshape(rows, width), (((0,), (0,)), ((), ())), preferred_element_type=F32
    )
    for o in range(1, nx):
        i = at_x(-o)
        sems.arrived(out_came[0] + i, shared_recv.at[i], along_x(i))
        total += shared_recv[i].astype(F32)
    out_ref[...] = total.astype(BF16)
    for copy in sems.started:
        copy.wait_send()
    for place, copy in shared_copies:
        pl.when(place != x)(copy.wait_send)


def on_device(nx, ndp, tokens, router, eg, eu, ed, sg, su, sd, ids, slots):
    toks, width = tokens.shape
    ny = ndp // 2
    cap = min(2 * toks // ny, toks // 2)
    rows = ny * cap
    units = eg.shape[1]
    hid = sg.shape[1]
    features = eg.shape[0]
    krows = sg.shape[0]
    half = nx // 2
    vmem = lambda *shape, dtype=BF16: pltpu.VMEM(shape, dtype)
    any_space = pl.BlockSpec(memory_space=pl.ANY)
    in_vmem = pl.BlockSpec(memory_space=pltpu.VMEM)
    return pl.pallas_call(
        functools.partial(kernel, (nx, ny, cap)),
        out_shape=jax.ShapeDtypeStruct((toks, width), BF16),
        in_specs=[in_vmem] * 2 + [any_space] * 8,
        out_specs=in_vmem,
        scratch_shapes=[
            vmem(nx, toks, width),
            vmem(router.shape[1], features),
            vmem(features, units),
            vmem(features, units),
            vmem(nx, units, width),
            vmem(ny, 2 * krows, hid),
            vmem(ny, 2 * krows, hid),
            vmem(ny, 2 * krows, hid),
            vmem(ny, cap, width),
            vmem(nx, 2 * rows, width),
            vmem(2 * rows, units, dtype=F32),
            vmem(2 * rows, units, dtype=F32),
            vmem(2 * rows, router.shape[1], dtype=F32),
            vmem(2 * rows, units),
            vmem(nx, rows, width, dtype=F32),
            vmem(nx, rows, width),
            vmem(nx, rows, width),
            vmem(2, half, rows, width),
            vmem(2, half, rows, width),
            vmem(rows, width),
            vmem(ny, cap, width),
            vmem(toks, hid, dtype=F32),
            vmem(toks, hid, dtype=F32),
            vmem(toks, hid),
            vmem(nx, toks, width),
            vmem(nx, toks, width),
            pltpu.SemaphoreType.DMA((192,)),
            pltpu.SemaphoreType.DMA((192,)),
            pltpu.SemaphoreType.DMA((32,)),
        ],
        compiler_params=pltpu.CompilerParams(
            collective_id=0, has_side_effects=True, vmem_limit_bytes=66_000_000
        ),
        name="layer",
    )(ids.reshape(1, toks), slots.reshape(1, toks), tokens, router.T, eg, eu, ed, sg, su, sd.T)


def solution(mesh):
    in_specs = (
        P(("group", "dp"), "tensor"),
        P(),
        P(None, ("dp", "tensor")),
        P(None, ("dp", "tensor")),
        P(("dp", "tensor"), None),
        P("dp", "tensor"),
        P("dp", "tensor"),
        P("tensor", "dp"),
        P(("group", "dp")),
        P(("group", "dp")),
    )
    return jax.shard_map(
        functools.partial(on_device, mesh.shape["tensor"], mesh.shape["dp"]),
        mesh=mesh,
        in_specs=in_specs,
        out_specs=P(("group", "dp"), "tensor"),
        check_vma=False,
    )
```

time: 343 us -> 140 us (0.41)
  the two profiles are of different devices: /device:TPU:513 before, /device:TPU:521 now
where the time goes in v1:
time: 140 us
  Pallas kernels  138 us (99%)
  local copies, waits for them, and re-layouts  1.6 us (1%)
    pallas_call x1, Pallas kernels, on_device(): pl.pallas_call(functools.partial(kernel, (nx, ny, cap)), out_shape=jax.Sh...  138 us

profile of v1, /device:TPU:521, one launch (start us, length us, event | category | flops | bytes accessed | tf_op | source)
XLA Modules:
  0.0 139.8 jit_solution(13801284470324165469)
XLA Ops:
  0.0 138.2 %layer.1 = bf16[128,640]{1,0:T(8,128)(2,1)} custom-call(s32[1,128]{1,0:T(1,128)} %bitcast.6, s32[1,128]{1,0:T(1,128)} %bitcast.7, bf16[128,640]{1,0:T(8,128)(2,1)} %tok_hbm.1, bf16[8,5120]{1,0:T(8,128)(2,1)} %bitcast.5, bf16[5120,256]{1,0:T(8,128)(2,1)} %eg_hbm.1, bf16[5120,256]{1,0:T(8,128)(2,1)} %eu_hbm.1, bf16[256,5120]{1,0:T(8,128)(2,1)} %ed_hbm.1, ...), custom_call_target="tpu_custom_call" | custom-call | tf_op jit(solution)/shard_map/layer/pallas_call | solution.py:472
  138.2 1.6 %copy.12 = bf16[128,640]{1,0:T(8,128)(2,1)} copy(bf16[128,640]{1,0:T(8,128)(2,1)} %layer.1) | data formatting | bytes 327680
